TPU v7x, 32 devices: a whole 2x2x4 slice. The times are simulated.
32 devices in a mesh: ta: 4 (over y, x), sa: 8 (over z, core).
Axes of the slice: x: 2, y: 2, z: 4, core: 2. Of those that a mesh axis runs over, the one named last changes fastest.
Arguments:
- eigvecs: float32 [2, 8, 64, 3, 4096], P(None, 'ta', None, None, 'sa'), may hold values from -0.0546875 to 0.0546875
- solutions: float32 [2, 8, 3, 8, 4, 3, 4096], P(None, 'ta', None, None, None, None, 'sa'), may hold values from -15 to 15
- source_times: int32 [3], replicated, may hold values from 0 to 7, as said below
- spin_dilution: int32 [3, 8], replicated, may hold values from 0 to 3
Outputs:
- perambulator: float32 [2, 8, 6144], P(None, 'ta', 'sa')
- norms: float32 [3, 8], replicated
Inputs may be any that keep to these rules, and one draw needn't show every extreme that they name: `source_times`: some source lies at slice 0 and another at slice 8 - 1.
All inputs are finite; a program needn't handle non-finite values.
Results may differ from a plain program's by a relative error of at most 0.000084.
Values sent between devices are 32-bit elements; how exact they have to be, the bound alone decides.
A program may use at most 64 MiB of HBM per device.

v0:
```python
import jax
import jax.numpy as jnp
from jax import lax
from jax.sharding import PartitionSpec as P


def on_device(eigvecs, solutions, source_times, spin_dilution):
    time_rows = eigvecs.shape[1]
    eig_count = eigvecs.shape[2]
    site_count = eigvecs.shape[4]
    src_count = spin_dilution.shape[0]
    col_count = spin_dilution.shape[1]
    columns = src_count * col_count * 4
    inner_len = 3 * site_count
    all_cells = 12.0 * time_rows * lax.axis_size("ta") * site_count * lax.axis_size("sa")
    norm_parts = jnp.sum(solutions * solutions, axis=(0, 1, 4, 5, 6))
    eigen_rows = eigvecs.reshape(2, time_rows, eig_count, inner_len)
    solution_rows = solutions.reshape(2, time_rows, columns, inner_len)
    precise = lax.Precision.HIGHEST
    upper_half = jnp.concatenate([eigen_rows[0], eigen_rows[1]], axis=2)
    lower_half = jnp.concatenate([-eigen_rows[1], eigen_rows[0]], axis=2)
    left_side = jnp.concatenate([upper_half, lower_half], axis=1)
    right_side = jnp.concatenate([solution_rows[0], solution_rows[1]], axis=2)
    stacked = jnp.einsum(
        "tmk,tnk->tmn", left_side, right_side, precision=precise, preferred_element_type=jnp.float32
    )
    real_part = stacked[:, :eig_count]
    imag_part = stacked[:, eig_count:]
    slice_times = lax.axis_index("ta") * time_rows + jnp.arange(time_rows, dtype=jnp.int32)
    boundary = jnp.where(slice_times[:, None] < source_times[None, :], -1.0, 1.0).astype(
        jnp.float32
    )
    chirality = jnp.where(spin_dilution < 2, 1.0, -1.0).astype(jnp.float32)
    signs = jnp.broadcast_to(
        (boundary[:, :, None] * chirality[None])[:, :, :, None],
        (time_rows, src_count, col_count, 4),
    ).reshape(time_rows, columns)
    partial_value = (jnp.stack([real_part, imag_part]) * signs[None, :, None, :]).reshape(
        2, time_rows, eig_count * columns
    )
    own_width = eig_count * columns // lax.axis_size("sa")
    own_start = lax.axis_index("sa") * own_width
    norm_total = lax.psum(norm_parts, ("ta", "sa"))
    summed = lax.psum(partial_value, "sa")
    perambulator = lax.dynamic_slice_in_dim(summed, own_start, own_width, 2)
    return (perambulator, norm_total / all_cells)


def solution(mesh):
    return jax.shard_map(
        on_device,
        mesh=mesh,
        in_specs=(
            P(None, "ta", None, None, "sa"),
            P(None, "ta", None, None, None, None, "sa"),
            P(),
            P(),
        ),
        out_specs=(P(None, "ta", "sa"), P()),
        check_vma=False,
    )
```

profile of v0, /device:TPU:0, one launch (start us, length us, event | category | flops | bytes accessed | tf_op | source)
XLA Modules:
  0.0 92.8 jit_solution(17779468733230858066)
XLA Ops:
  7.2 0.0 all-reduce.2.cloned.1.call-start
  7.2 0.0 copy-start
  7.2 3.3 %fusion.12 = (f32[1,2,3,8,4,3,512]{6,4,5,3,2,1,0:T(4,128)S(1)}, f32[1,2,3,8,4,3,512]{6,4,5,3,2,1,0:T(4,128)}) fusion(f32[2,2,3,8,4,3,512]{6,4,5,3,2,1,0:T(4,128)} %param.5), kind=kLoop, calls=%fused_computation.20 | loop fusion | bytes 4718592 | tf_op jit(solution)/shard_map/slice | solution.py:23
  10.6 0.0 copy-done
  10.6 0.0 copy-start.1
  10.6 0.6 multiply_reduce_fusion
  11.1 0.8 copy-done.1
  12.0 0.1 fusion.13
  12.1 0.5 copy.10
  12.6 1.5 %squeeze.14 = f32[2,64,1536]{2,1,0:T(8,128)} reshape(f32[1,2,64,3,512]{4,3,2,1,0:T(4,128)S(1)} %copy.10) | data formatting | bytes 1572864 | tf_op jit(solution)/shard_map/squeeze | solution.py:20
  14.1 0.5 copy.11
  14.7 0.6 squeeze.15
  15.3 0.9 %neg.3 = f32[2,64,1536]{2,1,0:T(8,128)} negate(f32[2,64,1536]{2,1,0:T(8,128)S(1)} %squeeze.15) | non-fusion elementwise | flops 196608 | bytes 1572864 | tf_op jit(solution)/shard_map/neg | solution.py:21
  16.2 1.9 %copy.13 = f32[1,2,3,8,4,3,512]{6,5,4,3,2,1,0:T(4,128)S(1)} copy(f32[1,2,3,8,4,3,512]{6,4,5,3,2,1,0:T(4,128)} %get-tuple-element.3) | data formatting | bytes 2359296 | tf_op jit(solution)/shard_map/slice | solution.py:23
  18.1 1.7 %squeeze.17 = f32[2,96,1536]{2,1,0:T(8,128)} reshape(f32[1,2,3,8,4,3,512]{6,5,4,3,2,1,0:T(4,128)S(1)} %copy.13) | data formatting | bytes 2359296 | tf_op jit(solution)/shard_map/squeeze | solution.py:23
  19.9 0.7 copy.12
  20.5 0.0 copy-start.2
  20.6 1.7 %squeeze.16 = f32[2,96,1536]{2,1,0:T(8,128)} reshape(f32[1,2,3,8,4,3,512]{6,5,4,3,2,1,0:T(4,128)S(1)} %copy.12) | data formatting | bytes 2359296 | tf_op jit(solution)/shard_map/squeeze | solution.py:23
  22.3 0.0 copy-done.2
  22.3 0.0 copy-start.3
  22.3 0.0 copy-start.4
  22.3 5.4 %fusion = f32[2,128,96]{1,2,0:T(8,128)S(1)} fusion(f32[2,64,1536]{2,1,0:T(8,128)} %squeeze.14, f32[2,64,1536]{2,1,0:T(8,128)} %neg.3, f32[2,64,1536]{2,1,0:T(8,128)S(1)} %squeeze.15, f32[2,96,1536]{2,1,0:T(8,128)S(1)} %copy-done.2, f32[2,96,1536]{2,1,0:T(8,128)} %squeeze.16), kind=kOutput, calls=%fused_computation | convolution fusion | flops 908918784 | bytes 4816896 | tf_op jit(solution)/shard_map/tmk,tnk->tmn/dot_general | solution.py:24
  27.6 0.1 fusion.14
  27.7 0.1 copy.15
  27.8 0.1 stack.10
  28.0 0.1 copy.14
  28.0 0.1 stack.9
  28.2 0.0 copy-done.3
  28.2 0.0 copy-done.4
  28.2 0.1 compare_select_fusion.1
  28.3 0.1 broadcast_multiply_fusion
  28.4 0.1 broadcast_in_dim.30
  28.4 0.1 mul.45
  28.6 0.1 mul.47
  28.7 0.7 maximum_multiply_fusion
  29.4 0.0 all-reduce.2.cloned.1.call-update
  29.4 42.0 %psum.15 = f32[3,8]{1,0:T(4,128)S(1)} all-reduce(f32[3,8]{1,0:T(4,128)S(1)} %multiply_reduce_fusion), channel_id=1, replica_groups=mesh['ta'=4,'sa'=8] {'ta','sa'}, use_global_device_ids=true, to_apply=%region_2.3 | all-reduce | flops 24 | bytes 192 | tf_op jit(solution)/shard_map/psum | solution.py:43
  71.4 0.6 broadcast_multiply_fusion.1
  72.0 12.7 %all-reduce.2.cloned.1.call-done = f32[2,2,6144]{2,1,0:T(2,128)} async-done(((f32[2,2,6144]{2,1,0:T(2,128)}), f32[2,2,6144]{2,1,0:T(2,128)}) %all-reduce.2.cloned.1.call-update) | async-done | bytes 98320 | tf_op jit(solution)/shard_map/psum | solution.py:44
  84.7 1.3 %constant_dynamic-slice_fusion = f32[2,2,768]{2,1,0:T(2,128)} fusion(f32[2,2,6144]{2,1,0:T(2,128)} %all-reduce.2.cloned.1.call-done, s32[]{:T(128)S(6)} %select_n.17), kind=kLoop, calls=%fused_computation.18 | loop fusion | bytes 24580 | tf_op jit(solution)/shard_map/dynamic_slice | solution.py:45
  (3 shorter events, 0.0 us)
Async XLA Ops:
  7.2 77.5 %all-reduce.2.cloned.1.call-start = ((), (), s32[]{:S(2)}) async-start(), calls=%async_computation | async-start | bytes 196608 | tf_op jit(solution)/shard_map/psum | solution.py:44
  7.2 3.3 %copy-start = (f32[2,2,3,8,4,3,512]{6,4,5,3,2,1,0:T(4,128)S(1)}, f32[2,2,3,8,4,3,512]{6,4,5,3,2,1,0:T(4,128)}, u32[]{:S(2)}) copy-start(f32[2,2,3,8,4,3,512]{6,4,5,3,2,1,0:T(4,128)} %param.5) | copy-start | bytes 7077892
  10.6 1.4 %copy-start.1 = (f32[2,2,64,3,512]{4,2,3,1,0:T(8,128)S(1)}, f32[2,2,64,3,512]{4,2,3,1,0:T(8,128)}, u32[]{:S(2)}) copy-start(f32[2,2,64,3,512]{4,2,3,1,0:T(8,128)} %param.4) | copy-start | bytes 4718596
  20.5 1.7 %copy-start.2 = (f32[2,96,1536]{2,1,0:T(8,128)S(1)}, f32[2,96,1536]{2,1,0:T(8,128)}, u32[]{:S(2)}) copy-start(f32[2,96,1536]{2,1,0:T(8,128)} %squeeze.17) | copy-start | bytes 3538948
  22.3 5.9 %copy-start.3 = (s32[3,8]{1,0:T(4,128)S(1)}, s32[3,8]{1,0:T(4,128)}, u32[]{:S(2)}) copy-start(s32[3,8]{1,0:T(4,128)} %param.7) | copy-start | bytes 292
  22.3 5.9 %copy-start.4 = (s32[3]{0:T(128)S(1)}, s32[3]{0:T(128)}, u32[]{:S(2)}) copy-start(s32[3]{0:T(128)} %param.6) | copy-start | bytes 40
Sparse Core Ops, SparseCore 0:
  29.5 55.1 all-reduce.1
where the time goes:
time: 93.2 us; the launch traced here: 92.8 us
  blocking collectives  42 us (45%)
  local copies, waits for them, and re-layouts  15.6 us (17%)
  between operations  14.2 us (15%)
  waiting for transfers between devices  12.7 us (14%)
  matrix products  5.36 us (6%)
  other arithmetic  2.95 us (3%)
    psum x1, blocking collectives, on_device(): norm_total = lax.psum(norm_parts, ('ta', 'sa'))  42 us
    psum x1, waiting for transfers between devices, on_device(): summed = lax.psum(partial_value, 'sa')  12.7 us
    slice x3, local copies, waits for them, and re-layouts, on_device(): right_side = jnp.concatenate([solution_rows[0], solution_rows[1]], axis=2)  5.92 us
    dot_general x1, matrix products, on_device(): jnp.einsum('tmk,tnk->tmn', left_side, right_side, precision=precise, pref...  5.36 us
    squeeze x2, local copies, waits for them, and re-layouts, on_device(): right_side = jnp.concatenate([solution_rows[0], solution_rows[1]], axis=2)  3.46 us
    squeeze x2, local copies, waits for them, and re-layouts, on_device(): upper_half = jnp.concatenate([eigen_rows[0], eigen_rows[1]], axis=2)  2.07 us
  transfers between devices with their start and end apart: 1, of which 1 were waited for; matrix products, arithmetic and copies ran while one was open for 1% of the time, Pallas kernels for 0%

commit v1 on v0

v1 whole, which is shorter than its diff:
```python
import functools
import math

import jax
import jax.numpy as jnp
from jax import lax
from jax.experimental import pallas as pl
from jax.experimental.pallas import tpu as pltpu
from jax.sharding import PartitionSpec as P

LANES = 128
NT_DIMS = (((1,), (1,)), ((), ()))


def split_two(x):
    high = x.astype(jnp.bfloat16)
    low = (x - high.astype(jnp.float32)).astype(jnp.bfloat16)
    return high, low


def kernel(
    dims,
    eig_hbm, sol_hbm, times_ref, spin_ref,
    out_ref, norm_ref,
    eig_buf, sol_buf, left, right_hi, right_lo, tile_buf, flat_buf,
    send_buf, recv_buf, norm_send, norm_recv,
    eig_sem, sol_sem, out_sems, in_sems, norm_out_sems, norm_in_sems,
):
    n_ta, n_sa, parts, slices, eigs, colors, sites, srcs, cols, spins, width = dims
    columns = srcs * cols * spins
    rows_own = width // LANES
    blocks = sites // LANES
    my_ta, my_sa = lax.axis_index("ta"), lax.axis_index("sa")

    barrier = pltpu.get_barrier_semaphore()
    for off in range(1, n_sa):
        pl.semaphore_signal(barrier, inc=1, device_id={"sa": lax.rem(my_sa + off, n_sa)})
    for off in range(1, n_ta):
        pl.semaphore_signal(barrier, inc=1, device_id={"ta": lax.rem(my_ta + off, n_ta)})

    sol_copies, eig_copies = {}, {}
    for t in range(slices):
        for c in range(colors):
            for j in range(blocks):
                at = (t * colors + c) * blocks + j
                copy = pltpu.make_async_copy(
                    sol_hbm.at[:, t, :, c, :, pl.ds(j * LANES, LANES)],
                    sol_buf.at[at].reshape(parts, srcs * cols, spins, LANES),
                    sol_sem.at[at],
                )
                copy.start()
                sol_copies[t, c, j] = copy
            copy = pltpu.make_async_copy(
                eig_hbm.at[:, t, c], eig_buf.at[t * colors + c], eig_sem.at[t * colors + c]
            )
            copy.start()
            eig_copies[t, c] = copy

    lane = lax.broadcasted_iota(jnp.int32, (8, LANES), 1)
    chir = jnp.ones((8, LANES), jnp.float32)
    group = lane // spins
    for s in range(srcs):
        for k in range(cols):
            value = jnp.where(spin_ref[s, k] < 2, 1.0, -1.0)
            chir = jnp.where(group == s * cols + k, value, chir)
    source = lane // (spins * cols)
    signs = []
    for t in range(slices):
        now = my_ta * slices + t
        sign = chir
        for s in range(srcs):
            value = jnp.where(now < times_ref[s], -1.0, 1.0)
            sign = jnp.where(source == s, chir * value, sign)
        signs.append(sign[:1])

    inner = colors * sites
    pad = LANES - columns
    if pad:
        for t in range(slices):
            for p in range(parts):
                rows = pl.ds(p * LANES + columns, pad)
                right_hi[t, rows, :] = jnp.zeros((pad, inner), jnp.bfloat16)
                right_lo[t, rows, :] = jnp.zeros((pad, inner), jnp.bfloat16)
    squares = jnp.zeros((columns, LANES), jnp.float32)
    for t in range(slices):
        for c in range(colors):
            for j in range(blocks):
                sol_copies[t, c, j].wait()
                lanes = pl.ds(c * sites + j * LANES, LANES)
                for p in range(parts):
                    x = sol_buf[(t * colors + c) * blocks + j, p]
                    squares = squares + x * x
                    high, low = split_two(x)
                    right_hi[t, pl.ds(p * LANES, columns), lanes] = high
                    right_lo[t, pl.ds(p * LANES, columns), lanes] = low
            eig_copies[t, c].wait()
            lanes = pl.ds(c * sites, sites)
            for p in range(parts):
                high, low = split_two(eig_buf[t * colors + c, p])
                left[t, pl.ds(p * eigs, eigs), lanes] = high
                left[t, pl.ds((parts + p) * eigs, eigs), lanes] = low

    pl.semaphore_wait(barrier, n_sa + n_ta - 2)

    precise = lax.Precision.HIGHEST
    lane_sums = lax.dot_general(
        jnp.ones((8, LANES), jnp.float32), squares, NT_DIMS,
        precision=precise, preferred_element_type=jnp.float32,
    )
    wanted = lax.broadcasted_iota(jnp.int32, (8, columns), 0)
    given = lax.broadcasted_iota(jnp.int32, (8, columns), 1)
    lane_sums = jnp.where(given // (spins * cols) == wanted, lane_sums, 0.0)
    col_of = lax.broadcasted_iota(jnp.int32, (LANES, columns), 0)
    col_in = lax.rem(lax.broadcasted_iota(jnp.int32, (LANES, columns), 1) // spins, cols)
    picks = jnp.where(col_of == col_in, 1.0, 0.0).astype(jnp.float32)
    norm_send[...] = lax.dot_general(
        lane_sums, picks, NT_DIMS, precision=precise, preferred_element_type=jnp.float32
    )
    norm_copies = []
    for off in range(1, n_ta):
        copy = pltpu.make_async_remote_copy(
            src_ref=norm_send,
            dst_ref=norm_recv.at[off - 1],
            send_sem=norm_out_sems.at[off - 1],
            recv_sem=norm_in_sems.at[off - 1],
            device_id={"ta": lax.rem(my_ta + off, n_ta)},
        )
        copy.start()
        norm_copies.append(copy)

    period = math.lcm(columns, LANES)
    rows_in, rows_out = period // columns, period // LANES
    groups = eigs // rows_in
    lane_g = lax.broadcasted_iota(jnp.int32, (groups, LANES), 1)
    copies = {}
    for t in range(slices):
        both = lax.dot_general(
            left[t], right_hi[t], NT_DIMS, preferred_element_type=jnp.float32
        )
        cross = lax.dot_general(
            left[t, : parts * eigs, :], right_lo[t], NT_DIMS,
            preferred_element_type=jnp.float32,
        )
        g = both[: parts * eigs] + both[parts * eigs :] + cross
        tiles = (
            g[:eigs, :LANES] + g[eigs:, LANES:],
            g[:eigs, LANES:] - g[eigs:, :LANES],
        )
        for p in range(parts):
            tile_buf[t, p] = tiles[p] * signs[t]
            rows = [tile_buf[t, p, pl.ds(i, groups, stride=rows_in), :] for i in range(rows_in)]
            for o in range(rows_out):
                value, filled = None, 0
                while filled < LANES:
                    i, skip = divmod(o * LANES + filled, columns)
                    size = min(columns - skip, LANES - filled)
                    shift = (filled - skip) % LANES
                    piece = pltpu.roll(rows[i], shift, 1) if shift else rows[i]
                    value = piece if value is None else jnp.where(lane_g < filled, value, piece)
                    filled += size
                flat_buf[t, p, pl.ds(o, groups, stride=rows_out), :] = value
            for d in range(n_sa):
                send_buf[t, d, pl.ds(p * rows_own, rows_own), :] = flat_buf[
                    t, p, pl.ds(d * rows_own, rows_own), :
                ]
        if t == slices - 1:
            norm = norm_send[...]
            for off in range(1, n_ta):
                norm_copies[off - 1].wait_recv()
                norm = norm + norm_recv[off - 1]
            for d in range(n_sa):
                send_buf[t, d, pl.ds(parts * rows_own, srcs), :] = norm[:srcs]
        for off in range(1, n_sa):
            peer = lax.rem(my_sa + off, n_sa)
            copy = pltpu.make_async_remote_copy(
                src_ref=send_buf.at[t, peer],
                dst_ref=recv_buf.at[t, off - 1],
                send_sem=out_sems.at[t, off - 1],
                recv_sem=in_sems.at[t, off - 1],
                device_id={"sa": peer},
            )
            copy.start()
            copies[t, off] = copy

    for t in range(slices):
        total = send_buf[t, my_sa]
        for off in range(1, n_sa):
            copies[t, off].wait_recv()
            total = total + recv_buf[t, off - 1]
        for p in range(parts):
            for r in range(rows_own):
                row = p * rows_own + r
                out_ref[p, pl.ds(t, 1), pl.ds(r * LANES, LANES)] = total[row : row + 1]
        if t == slices - 1:
            cells = 1.0 * spins * colors * slices * n_ta * sites * n_sa
            at = parts * rows_own
            norm_ref[...] = total[at : at + srcs, :cols] / cells
    for copy in norm_copies:
        copy.wait_send()
    for copy in copies.values():
        copy.wait_send()


def on_device(eigvecs, solutions, source_times, spin_dilution):
    n_ta, n_sa = lax.axis_size("ta"), lax.axis_size("sa")
    parts, slices, eigs, colors, sites = eigvecs.shape
    _, _, srcs, cols, spins, _, _ = solutions.shape
    columns = srcs * cols * spins
    width = eigs * columns // n_sa
    eig_view = jnp.transpose(eigvecs, (0, 1, 3, 2, 4))
    sol_view = jnp.transpose(solutions, (0, 1, 2, 3, 5, 4, 6)).reshape(
        parts, slices, srcs * cols, colors, spins, sites
    )
    dims = (n_ta, n_sa, parts, slices, eigs, colors, sites, srcs, cols, spins, width)
    blocks = sites // LANES
    inner = colors * sites
    rows = -(-(parts * (width // LANES) + srcs) // 8) * 8
    f32, bf16 = jnp.float32, jnp.bfloat16
    dma = pltpu.SemaphoreType.DMA
    return pl.pallas_call(
        functools.partial(kernel, dims),
        out_shape=(
            jax.ShapeDtypeStruct((parts, slices, width), f32),
            jax.ShapeDtypeStruct((srcs, cols), f32),
        ),
        in_specs=[
            pl.BlockSpec(memory_space=pltpu.HBM),
            pl.BlockSpec(memory_space=pltpu.HBM),
            pl.BlockSpec(memory_space=pltpu.SMEM),
            pl.BlockSpec(memory_space=pltpu.SMEM),
        ],
        out_specs=(
            pl.BlockSpec(memory_space=pltpu.VMEM),
            pl.BlockSpec(memory_space=pltpu.VMEM),
        ),
        scratch_shapes=[
            pltpu.VMEM((slices * colors, parts, eigs, sites), f32),
            pltpu.VMEM((slices * colors * blocks, parts, columns, LANES), f32),
            pltpu.VMEM((slices, 2 * parts * eigs, inner), bf16),
            pltpu.VMEM((slices, parts * LANES, inner), bf16),
            pltpu.VMEM((slices, parts * LANES, inner), bf16),
            pltpu.VMEM((slices, parts, eigs, LANES), f32),
            pltpu.VMEM((slices, parts, eigs * columns // LANES, LANES), f32),
            pltpu.VMEM((slices, n_sa, rows, LANES), f32),
            pltpu.VMEM((slices, n_sa - 1, rows, LANES), f32),
            pltpu.VMEM((8, LANES), f32),
            pltpu.VMEM((n_ta - 1, 8, LANES), f32),
            dma((slices * colors,)),
            dma((slices * colors * blocks,)),
            dma((slices, n_sa - 1)),
            dma((slices, n_sa - 1)),
            dma((n_ta - 1,)),
            dma((n_ta - 1,)),
        ],
        compiler_params=pltpu.CompilerParams(collective_id=0, has_side_effects=True),
    )(eig_view, sol_view, source_times, spin_dilution)


def solution(mesh):
    return jax.shard_map(
        on_device,
        mesh=mesh,
        in_specs=(
            P(None, "ta", None, None, "sa"),
            P(None, "ta", None, None, None, None, "sa"),
            P(),
            P(),
        ),
        out_specs=(P(None, "ta", "sa"), P()),
        check_vma=False,
    )
```

time: 93.2 us -> 19 us (0.20)
  blocking collectives: 42 us -> 0 us
  Pallas kernels: 0 us -> 15.6 us
  between operations: 14.2 us -> 0.64 us
  local copies, waits for them, and re-layouts: 15.6 us -> 2.54 us
  waiting for transfers between devices: 12.7 us -> 0 us
  matrix products: 5.36 us -> 0 us
  other arithmetic: 2.95 us -> 0 us
    psum x1 -> x0, blocking collectives: 42 us -> none  [on_device(): norm_total = lax.psum(norm_parts, ('ta', 'sa'))]
    pallas_call x0 -> x1, Pallas kernels: none -> 15.6 us  [on_device(): pl.pallas_call(functools.partial(kernel, dims), out_shape=(jax.ShapeDtype...]
    psum x1 -> x0, waiting for transfers between devices: 12.7 us -> none  [on_device(): summed = lax.psum(partial_value, 'sa')]
    slice x9 -> x0, local copies, waits for them, and re-layouts: 7.37 us -> none  [the longest x3 5.92 us: on_device(): right_side = jnp.concatenate([solution_rows[0], solution_rows[1]], axis=2)]
    squeeze x4 -> x0, local copies, waits for them, and re-layouts: 5.53 us -> none  [the longest x2 3.46 us: on_device(): right_side = jnp.concatenate([solution_rows[0], solution_rows[1]], axis=2)]
    dot_general x1 -> x0, matrix products: 5.36 us -> none  [on_device(): jnp.einsum('tmk,tnk->tmn', left_side, right_side, precision=precise, pref...]
    unnamed x10 -> x2, local copies, waits for them, and re-layouts: 0.83 us -> 2.54 us
    dynamic_slice x1 -> x0, local copies, waits for them, and re-layouts: 1.31 us -> none  [on_device(): perambulator = lax.dynamic_slice_in_dim(summed, own_start, own_width, 2)]
  transfers between devices with their start and end apart: 1 -> 0, of which waited for: 1 -> 0; matrix products, arithmetic and copies ran while one was open for 1% -> 0% of each run, Pallas kernels for 0% -> 0%
where the time goes in v1:
time: 19 us; the launch traced here: 18.7 us
  Pallas kernels  15.6 us (82%)
  local copies, waits for them, and re-layouts  2.54 us (13%)
  between operations  0.64 us (3%)
    pallas_call x1, Pallas kernels, on_device(): pl.pallas_call(functools.partial(kernel, dims), out_shape=(jax.ShapeDtype...  15.6 us
    unnamed x2, local copies, waits for them, and re-layouts  2.54 us

profile of v1, /device:TPU:0, one launch (start us, length us, event | category | flops | bytes accessed | tf_op | source)
XLA Modules:
  0.0 18.7 jit_solution(14542882843633630162)
XLA Ops:
  0.6 15.6 %shard_map.59 = (f32[2,2,768]{2,1,0:T(2,128)}, f32[3,8]{1,0:T(4,128)}) custom-call(f32[2,2,3,64,512]{4,3,2,1,0:T(8,128)} %bitcast.5, f32[2,2,24,3,4,512]{5,4,3,2,1,0:T(4,128)} %bitcast.4, s32[3]{0:T(128)} %times_ref.1, s32[3,8]{1,0:T(4,128)} %spin_ref.1), custom_call_target="tpu_custom_call" | custom-call | tf_op jit(solution)/shard_map/pallas_call | solution.py:220
  16.2 1.3 %copy.8 = f32[2,2,768]{2,1,0:T(2,128)} copy(f32[2,2,768]{2,1,0:T(2,128)} %get-tuple-element.4) | data formatting | bytes 24576
  17.5 1.2 %copy.9 = f32[3,8]{1,0:T(4,128)} copy(f32[3,8]{1,0:T(4,128)} %get-tuple-element.5) | data formatting | bytes 192

commit v2 on v1

--- a/solution.py
+++ b/solution.py
@@ -20,11 +20,12 @@
 
 def kernel(
     dims,
-    eig_hbm, sol_hbm, times_ref, spin_ref,
+    eig_hbm, sol_hbm, times_hbm, spin_hbm,
     out_ref, norm_ref,
     eig_buf, sol_buf, left, right_hi, right_lo, tile_buf, flat_buf,
-    send_buf, recv_buf, norm_send, norm_recv,
-    eig_sem, sol_sem, out_sems, in_sems, norm_out_sems, norm_in_sems,
+    send_buf, recv_buf, norm_sa_send, norm_sa_recv, norm_ta_send, norm_ta_recv,
+    times_ref, spin_ref, small_sem, own_sem,
+    eig_sem, sol_sem, out_sems, in_sems, sa_out_sems, sa_in_sems, ta_out_sems, ta_in_sems,
 ):
     n_ta, n_sa, parts, slices, eigs, colors, sites, srcs, cols, spins, width = dims
     columns = srcs * cols * spins
@@ -38,6 +39,12 @@
     for off in range(1, n_ta):
         pl.semaphore_signal(barrier, inc=1, device_id={"ta": lax.rem(my_ta + off, n_ta)})
 
+    small_copies = [
+        pltpu.make_async_copy(times_hbm, times_ref, small_sem.at[0]),
+        pltpu.make_async_copy(spin_hbm, spin_ref, small_sem.at[1]),
+    ]
+    for copy in small_copies:
+        copy.start()
     sol_copies, eig_copies = {}, {}
     for t in range(slices):
         for c in range(colors):
@@ -55,23 +62,6 @@
             )
             copy.start()
             eig_copies[t, c] = copy
-
-    lane = lax.broadcasted_iota(jnp.int32, (8, LANES), 1)
-    chir = jnp.ones((8, LANES), jnp.float32)
-    group = lane // spins
-    for s in range(srcs):
-        for k in range(cols):
-            value = jnp.where(spin_ref[s, k] < 2, 1.0, -1.0)
-            chir = jnp.where(group == s * cols + k, value, chir)
-    source = lane // (spins * cols)
-    signs = []
-    for t in range(slices):
-        now = my_ta * slices + t
-        sign = chir
-        for s in range(srcs):
-            value = jnp.where(now < times_ref[s], -1.0, 1.0)
-            sign = jnp.where(source == s, chir * value, sign)
-        signs.append(sign[:1])
 
     inner = colors * sites
     pad = LANES - columns
@@ -107,32 +97,51 @@
         jnp.ones((8, LANES), jnp.float32), squares, NT_DIMS,
         precision=precise, preferred_element_type=jnp.float32,
     )
-    wanted = lax.broadcasted_iota(jnp.int32, (8, columns), 0)
-    given = lax.broadcasted_iota(jnp.int32, (8, columns), 1)
-    lane_sums = jnp.where(given // (spins * cols) == wanted, lane_sums, 0.0)
-    col_of = lax.broadcasted_iota(jnp.int32, (LANES, columns), 0)
-    col_in = lax.rem(lax.broadcasted_iota(jnp.int32, (LANES, columns), 1) // spins, cols)
-    picks = jnp.where(col_of == col_in, 1.0, 0.0).astype(jnp.float32)
-    norm_send[...] = lax.dot_general(
+    wanted = lax.broadcasted_iota(jnp.int32, (LANES, columns), 0)
+    given = lax.broadcasted_iota(jnp.int32, (LANES, columns), 1) // spins
+    picks = jnp.where(wanted == given, 1.0, 0.0).astype(jnp.float32)
+    own_norm = lax.dot_general(
         lane_sums, picks, NT_DIMS, precision=precise, preferred_element_type=jnp.float32
-    )
-    norm_copies = []
-    for off in range(1, n_ta):
+    )[:1]
+    norm_sa_send[...] = own_norm
+    norm_sa_copies, norm_ta_copies = [], []
+    for off in range(1, n_sa):
         copy = pltpu.make_async_remote_copy(
-            src_ref=norm_send,
-            dst_ref=norm_recv.at[off - 1],
-            send_sem=norm_out_sems.at[off - 1],
-            recv_sem=norm_in_sems.at[off - 1],
-            device_id={"ta": lax.rem(my_ta + off, n_ta)},
+            src_ref=norm_sa_send,
+            dst_ref=norm_sa_recv.at[off - 1],
+            send_sem=sa_out_sems.at[off - 1],
+            recv_sem=sa_in_sems.at[off - 1],
+            device_id={"sa": lax.rem(my_sa + off, n_sa)},
         )
         copy.start()
-        norm_copies.append(copy)
+        norm_sa_copies.append(copy)
+
+    for copy in small_copies:
+        copy.wait()
+    lane = lax.broadcasted_iota(jnp.int32, (8, LANES), 1)
+    chir = jnp.ones((8, LANES), jnp.float32)
+    group = lane // spins
+    for s in range(srcs):
+        for k in range(cols):
+            value = jnp.where(spin_ref[s, k] < 2, 1.0, -1.0)
+            chir = jnp.where(group == s * cols + k, value, chir)
+    source = lane // (spins * cols)
+    signs = []
+    for t in range(slices):
+        now = my_ta * slices + t
+        sign = chir
+        for s in range(srcs):
+            value = jnp.where(now < times_ref[s], -1.0, 1.0)
+            sign = jnp.where(source == s, chir * value, sign)
+        signs.append(sign[:1])
 
     period = math.lcm(columns, LANES)
     rows_in, rows_out = period // columns, period // LANES
     groups = eigs // rows_in
     lane_g = lax.broadcasted_iota(jnp.int32, (groups, LANES), 1)
-    copies = {}
+    copies, owns = {}, []
+    rows = parts * rows_own
+    sub = math.gcd(rows, 4)
     for t in range(slices):
         both = lax.dot_general(
             left[t], right_hi[t], NT_DIMS, preferred_element_type=jnp.float32
@@ -148,57 +157,79 @@
         )
         for p in range(parts):
             tile_buf[t, p] = tiles[p] * signs[t]
-            rows = [tile_buf[t, p, pl.ds(i, groups, stride=rows_in), :] for i in range(rows_in)]
+            taken = [tile_buf[t, p, pl.ds(i, groups, stride=rows_in), :] for i in range(rows_in)]
             for o in range(rows_out):
                 value, filled = None, 0
                 while filled < LANES:
                     i, skip = divmod(o * LANES + filled, columns)
                     size = min(columns - skip, LANES - filled)
                     shift = (filled - skip) % LANES
-                    piece = pltpu.roll(rows[i], shift, 1) if shift else rows[i]
+                    piece = pltpu.roll(taken[i], shift, 1) if shift else taken[i]
                     value = piece if value is None else jnp.where(lane_g < filled, value, piece)
                     filled += size
                 flat_buf[t, p, pl.ds(o, groups, stride=rows_out), :] = value
             for d in range(n_sa):
-                send_buf[t, d, pl.ds(p * rows_own, rows_own), :] = flat_buf[
+                send_buf[t, pl.ds(d * rows + p * rows_own, rows_own), :] = flat_buf[
                     t, p, pl.ds(d * rows_own, rows_own), :
                 ]
-        if t == slices - 1:
-            norm = norm_send[...]
-            for off in range(1, n_ta):
-                norm_copies[off - 1].wait_recv()
-                norm = norm + norm_recv[off - 1]
-            for d in range(n_sa):
-                send_buf[t, d, pl.ds(parts * rows_own, srcs), :] = norm[:srcs]
+        sent = send_buf.at[t].reshape(n_sa, rows // sub, sub, LANES)
+        landed = recv_buf.at[t].reshape(n_sa, rows // sub, sub, LANES)
         for off in range(1, n_sa):
             peer = lax.rem(my_sa + off, n_sa)
             copy = pltpu.make_async_remote_copy(
-                src_ref=send_buf.at[t, peer],
-                dst_ref=recv_buf.at[t, off - 1],
+                src_ref=sent.at[peer],
+                dst_ref=landed.at[off - 1],
                 send_sem=out_sems.at[t, off - 1],
                 recv_sem=in_sems.at[t, off - 1],
                 device_id={"sa": peer},
             )
             copy.start()
             copies[t, off] = copy
-
-    for t in range(slices):
-        total = send_buf[t, my_sa]
+        own = pltpu.make_async_copy(sent.at[my_sa], landed.at[n_sa - 1], own_sem.at[t])
+        own.start()
+        owns.append(own)
+
+    for off in range(1, n_sa):
+        norm_sa_copies[off - 1].wait_recv()
+        own_norm = own_norm + norm_sa_recv[off - 1]
+    norm_ta_send[...] = own_norm
+    for off in range(1, n_ta):
+        copy = pltpu.make_async_remote_copy(
+            src_ref=norm_ta_send,
+            dst_ref=norm_ta_recv.at[off - 1],
+            send_sem=ta_out_sems.at[off - 1],
+            recv_sem=ta_in_sems.at[off - 1],
+            device_id={"ta": lax.rem(my_ta + off, n_ta)},
+        )
+        copy.start()
+        norm_ta_copies.append(copy)
+
+    for t in range(slices):
+        owns[t].wait()
+        total = recv_buf[t, pl.ds((n_sa - 1) * rows, rows), :]
         for off in range(1, n_sa):
             copies[t, off].wait_recv()
-            total = total + recv_buf[t, off - 1]
+            total = total + recv_buf[t, pl.ds((off - 1) * rows, rows), :]
         for p in range(parts):
             for r in range(rows_own):
                 row = p * rows_own + r
                 out_ref[p, pl.ds(t, 1), pl.ds(r * LANES, LANES)] = total[row : row + 1]
-        if t == slices - 1:
-            cells = 1.0 * spins * colors * slices * n_ta * sites * n_sa
-            at = parts * rows_own
-            norm_ref[...] = total[at : at + srcs, :cols] / cells
-    for copy in norm_copies:
+    for off in range(1, n_ta):
+        norm_ta_copies[off - 1].wait_recv()
+        own_norm = own_norm + norm_ta_recv[off - 1]
+    cells = 1.0 * spins * colors * slices * n_ta * sites * n_sa
+    own_norm = own_norm / cells
+    for s in range(srcs):
+        norm_ref[pl.ds(s, 1), :] = own_norm[:, s * cols : (s + 1) * cols]
+    for copy in norm_sa_copies + norm_ta_copies:
         copy.wait_send()
     for copy in copies.values():
         copy.wait_send()
+
+
+def hand_over(tiles_ref, norms_ref, out_ref, norm_ref):
+    out_ref[...] = tiles_ref[...]
+    norm_ref[...] = norms_ref[...]
 
 
 def on_device(eigvecs, solutions, source_times, spin_dilution):
@@ -214,10 +245,10 @@
     dims = (n_ta, n_sa, parts, slices, eigs, colors, sites, srcs, cols, spins, width)
     blocks = sites // LANES
     inner = colors * sites
-    rows = -(-(parts * (width // LANES) + srcs) // 8) * 8
+    rows = parts * (width // LANES)
     f32, bf16 = jnp.float32, jnp.bfloat16
     dma = pltpu.SemaphoreType.DMA
-    return pl.pallas_call(
+    tiles, norms = pl.pallas_call(
         functools.partial(kernel, dims),
         out_shape=(
             jax.ShapeDtypeStruct((parts, slices, width), f32),
@@ -226,8 +257,8 @@
         in_specs=[
             pl.BlockSpec(memory_space=pltpu.HBM),
             pl.BlockSpec(memory_space=pltpu.HBM),
-            pl.BlockSpec(memory_space=pltpu.SMEM),
-            pl.BlockSpec(memory_space=pltpu.SMEM),
+            pl.BlockSpec(memory_space=pltpu.HBM),
+            pl.BlockSpec(memory_space=pltpu.HBM),
         ],
         out_specs=(
             pl.BlockSpec(memory_space=pltpu.VMEM),
@@ -241,19 +272,34 @@
             pltpu.VMEM((slices, parts * LANES, inner), bf16),
             pltpu.VMEM((slices, parts, eigs, LANES), f32),
             pltpu.VMEM((slices, parts, eigs * columns // LANES, LANES), f32),
-            pltpu.VMEM((slices, n_sa, rows, LANES), f32),
-            pltpu.VMEM((slices, n_sa - 1, rows, LANES), f32),
-            pltpu.VMEM((8, LANES), f32),
-            pltpu.VMEM((n_ta - 1, 8, LANES), f32),
+            pltpu.VMEM((slices, n_sa * rows, LANES), f32),
+            pltpu.VMEM((slices, n_sa * rows, LANES), f32),
+            pltpu.VMEM((1, LANES), f32),
+            pltpu.VMEM((n_sa - 1, 1, LANES), f32),
+            pltpu.VMEM((1, LANES), f32),
+            pltpu.VMEM((n_ta - 1, 1, LANES), f32),
+            pltpu.SMEM((srcs,), jnp.int32),
+            pltpu.SMEM((srcs, cols), jnp.int32),
+            dma((2,)),
+            dma((slices,)),
             dma((slices * colors,)),
             dma((slices * colors * blocks,)),
             dma((slices, n_sa - 1)),
             dma((slices, n_sa - 1)),
+            dma((n_sa - 1,)),
+            dma((n_sa - 1,)),
             dma((n_ta - 1,)),
             dma((n_ta - 1,)),
         ],
         compiler_params=pltpu.CompilerParams(collective_id=0, has_side_effects=True),
     )(eig_view, sol_view, source_times, spin_dilution)
+    return pl.pallas_call(
+        hand_over,
+        out_shape=(
+            jax.ShapeDtypeStruct(tiles.shape, f32),
+            jax.ShapeDtypeStruct(norms.shape, f32),
+        ),
+    )(tiles, norms)
 
 
 def solution(mesh):

time: 19 us -> 17.1 us (0.900)
  local copies, waits for them, and re-layouts: 2.54 us -> 0 us
  Pallas kernels: 15.6 us -> 16.3 us
    unnamed x2 -> x0, local copies, waits for them, and re-layouts: 2.54 us -> none
    pallas_call x0 -> x1, Pallas kernels: none -> 1.31 us  [on_device(): pl.pallas_call(hand_over, out_shape=(jax.ShapeDtypeStruct(tiles.shape, f3...]
    pallas_call x1, Pallas kernels: 15.6 us -> 15 us  [on_device(): pl.pallas_call(functools.partial(kernel, dims), out_shape=(jax.ShapeDtype...]
where the time goes in v2:
time: 17.1 us; the launch traced here: 16.9 us
  Pallas kernels  16.3 us (95%)
  between operations  0.64 us (4%)
    pallas_call x1, Pallas kernels, on_device(): pl.pallas_call(functools.partial(kernel, dims), out_shape=(jax.ShapeDtype...  15 us
    pallas_call x1, Pallas kernels, on_device(): pl.pallas_call(hand_over, out_shape=(jax.ShapeDtypeStruct(tiles.shape, f3...  1.31 us

profile of v2, /device:TPU:0, one launch (start us, length us, event | category | flops | bytes accessed | tf_op | source)
XLA Modules:
  0.0 16.9 jit_solution(6126074379085426740)
XLA Ops:
  0.6 15.0 %shard_map.59 = (f32[2,2,768]{2,1,0:T(2,128)}, f32[3,8]{1,0:T(4,128)}) custom-call(f32[2,2,3,64,512]{4,3,2,1,0:T(8,128)} %bitcast.5, f32[2,2,24,3,4,512]{5,4,3,2,1,0:T(4,128)} %bitcast.4, s32[3]{0:T(128)} %times_hbm.1, s32[3,8]{1,0:T(4,128)} %spin_hbm.1), custom_call_target="tpu_custom_call" | custom-call | tf_op jit(solution)/shard_map/pallas_call | solution.py:251
  15.6 1.3 %shard_map.60 = (f32[2,2,768]{2,1,0:T(2,128)}, f32[3,8]{1,0:T(4,128)}) custom-call(f32[2,2,768]{2,1,0:T(2,128)} %get-tuple-element.4.tiles_ref, f32[3,8]{1,0:T(4,128)} %get-tuple-element.5.norms_ref), custom_call_target="tpu_custom_call" | custom-call | tf_op jit(solution)/shard_map/pallas_call | solution.py:296

commit v3 on v2

--- a/solution.py
+++ b/solution.py
@@ -9,6 +9,7 @@
 from jax.sharding import PartitionSpec as P
 
 LANES = 128
+DIRECT = 64
 NT_DIMS = (((1,), (1,)), ((), ()))
 
 
@@ -23,9 +24,9 @@
     eig_hbm, sol_hbm, times_hbm, spin_hbm,
     out_ref, norm_ref,
     eig_buf, sol_buf, left, right_hi, right_lo, tile_buf, flat_buf,
-    send_buf, recv_buf, norm_sa_send, norm_sa_recv, norm_ta_send, norm_ta_recv,
+    send_buf, recv_buf, norm_send, norm_recv,
     times_ref, spin_ref, small_sem, own_sem,
-    eig_sem, sol_sem, out_sems, in_sems, sa_out_sems, sa_in_sems, ta_out_sems, ta_in_sems,
+    eig_sem, sol_sem, out_sems, in_sems, norm_out_sems, norm_in_sems,
 ):
     n_ta, n_sa, parts, slices, eigs, colors, sites, srcs, cols, spins, width = dims
     columns = srcs * cols * spins
@@ -34,10 +35,20 @@
     my_ta, my_sa = lax.axis_index("ta"), lax.axis_index("sa")
 
     barrier = pltpu.get_barrier_semaphore()
-    for off in range(1, n_sa):
-        pl.semaphore_signal(barrier, inc=1, device_id={"sa": lax.rem(my_sa + off, n_sa)})
-    for off in range(1, n_ta):
-        pl.semaphore_signal(barrier, inc=1, device_id={"ta": lax.rem(my_ta + off, n_ta)})
+    one_phase = n_ta * n_sa <= DIRECT
+    every = [(a, b) for a in range(n_ta) for b in range(n_sa) if a or b]
+    over_sa = [(0, b) for b in range(1, n_sa)]
+    over_ta = [(a, 0) for a in range(1, n_ta)]
+    first, second = (every, []) if one_phase else (over_sa, over_ta)
+
+    def device(offs):
+        return {
+            "ta": lax.rem(my_ta + offs[0], n_ta),
+            "sa": lax.rem(my_sa + offs[1], n_sa),
+        }
+
+    for offs in first + second:
+        pl.semaphore_signal(barrier, inc=1, device_id=device(offs))
 
     small_copies = [
         pltpu.make_async_copy(times_hbm, times_ref, small_sem.at[0]),
@@ -63,59 +74,6 @@
             copy.start()
             eig_copies[t, c] = copy
 
-    inner = colors * sites
-    pad = LANES - columns
-    if pad:
-        for t in range(slices):
-            for p in range(parts):
-                rows = pl.ds(p * LANES + columns, pad)
-                right_hi[t, rows, :] = jnp.zeros((pad, inner), jnp.bfloat16)
-                right_lo[t, rows, :] = jnp.zeros((pad, inner), jnp.bfloat16)
-    squares = jnp.zeros((columns, LANES), jnp.float32)
-    for t in range(slices):
-        for c in range(colors):
-            for j in range(blocks):
-                sol_copies[t, c, j].wait()
-                lanes = pl.ds(c * sites + j * LANES, LANES)
-                for p in range(parts):
-                    x = sol_buf[(t * colors + c) * blocks + j, p]
-                    squares = squares + x * x
-                    high, low = split_two(x)
-                    right_hi[t, pl.ds(p * LANES, columns), lanes] = high
-                    right_lo[t, pl.ds(p * LANES, columns), lanes] = low
-            eig_copies[t, c].wait()
-            lanes = pl.ds(c * sites, sites)
-            for p in range(parts):
-                high, low = split_two(eig_buf[t * colors + c, p])
-                left[t, pl.ds(p * eigs, eigs), lanes] = high
-                left[t, pl.ds((parts + p) * eigs, eigs), lanes] = low
-
-    pl.semaphore_wait(barrier, n_sa + n_ta - 2)
-
-    precise = lax.Precision.HIGHEST
-    lane_sums = lax.dot_general(
-        jnp.ones((8, LANES), jnp.float32), squares, NT_DIMS,
-        precision=precise, preferred_element_type=jnp.float32,
-    )
-    wanted = lax.broadcasted_iota(jnp.int32, (LANES, columns), 0)
-    given = lax.broadcasted_iota(jnp.int32, (LANES, columns), 1) // spins
-    picks = jnp.where(wanted == given, 1.0, 0.0).astype(jnp.float32)
-    own_norm = lax.dot_general(
-        lane_sums, picks, NT_DIMS, precision=precise, preferred_element_type=jnp.float32
-    )[:1]
-    norm_sa_send[...] = own_norm
-    norm_sa_copies, norm_ta_copies = [], []
-    for off in range(1, n_sa):
-        copy = pltpu.make_async_remote_copy(
-            src_ref=norm_sa_send,
-            dst_ref=norm_sa_recv.at[off - 1],
-            send_sem=sa_out_sems.at[off - 1],
-            recv_sem=sa_in_sems.at[off - 1],
-            device_id={"sa": lax.rem(my_sa + off, n_sa)},
-        )
-        copy.start()
-        norm_sa_copies.append(copy)
-
     for copy in small_copies:
         copy.wait()
     lane = lax.broadcasted_iota(jnp.int32, (8, LANES), 1)
@@ -142,7 +100,8 @@
     copies, owns = {}, []
     rows = parts * rows_own
     sub = math.gcd(rows, 4)
-    for t in range(slices):
+
+    def make_tiles(t):
         both = lax.dot_general(
             left[t], right_hi[t], NT_DIMS, preferred_element_type=jnp.float32
         )
@@ -172,6 +131,8 @@
                 send_buf[t, pl.ds(d * rows + p * rows_own, rows_own), :] = flat_buf[
                     t, p, pl.ds(d * rows_own, rows_own), :
                 ]
+
+    def send_tiles(t):
         sent = send_buf.at[t].reshape(n_sa, rows // sub, sub, LANES)
         landed = recv_buf.at[t].reshape(n_sa, rows // sub, sub, LANES)
         for off in range(1, n_sa):
@@ -189,20 +150,76 @@
         own.start()
         owns.append(own)
 
-    for off in range(1, n_sa):
-        norm_sa_copies[off - 1].wait_recv()
-        own_norm = own_norm + norm_sa_recv[off - 1]
-    norm_ta_send[...] = own_norm
-    for off in range(1, n_ta):
-        copy = pltpu.make_async_remote_copy(
-            src_ref=norm_ta_send,
-            dst_ref=norm_ta_recv.at[off - 1],
-            send_sem=ta_out_sems.at[off - 1],
-            recv_sem=ta_in_sems.at[off - 1],
-            device_id={"ta": lax.rem(my_ta + off, n_ta)},
-        )
-        copy.start()
-        norm_ta_copies.append(copy)
+    inner = colors * sites
+    pad = LANES - columns
+    if pad:
+        for t in range(slices):
+            for p in range(parts):
+                spare = pl.ds(p * LANES + columns, pad)
+                right_hi[t, spare, :] = jnp.zeros((pad, inner), jnp.bfloat16)
+                right_lo[t, spare, :] = jnp.zeros((pad, inner), jnp.bfloat16)
+    squares = jnp.zeros((columns, LANES), jnp.float32)
+    for t in range(slices):
+        for c in range(colors):
+            for j in range(blocks):
+                sol_copies[t, c, j].wait()
+                lanes = pl.ds(c * sites + j * LANES, LANES)
+                for p in range(parts):
+                    x = sol_buf[(t * colors + c) * blocks + j, p]
+                    squares = squares + x * x
+                    high, low = split_two(x)
+                    right_hi[t, pl.ds(p * LANES, columns), lanes] = high
+                    right_lo[t, pl.ds(p * LANES, columns), lanes] = low
+            eig_copies[t, c].wait()
+            lanes = pl.ds(c * sites, sites)
+            for p in range(parts):
+                high, low = split_two(eig_buf[t * colors + c, p])
+                left[t, pl.ds(p * eigs, eigs), lanes] = high
+                left[t, pl.ds((parts + p) * eigs, eigs), lanes] = low
+        if t < slices - 1:
+            make_tiles(t)
+
+    pl.semaphore_wait(barrier, len(first + second))
+
+    precise = lax.Precision.HIGHEST
+    lane_sums = lax.dot_general(
+        jnp.ones((8, LANES), jnp.float32), squares, NT_DIMS,
+        precision=precise, preferred_element_type=jnp.float32,
+    )
+    wanted = lax.broadcasted_iota(jnp.int32, (LANES, columns), 0)
+    given = lax.broadcasted_iota(jnp.int32, (LANES, columns), 1) // spins
+    picks = jnp.where(wanted == given, 1.0, 0.0).astype(jnp.float32)
+    own_norm = lax.dot_general(
+        lane_sums, picks, NT_DIMS, precision=precise, preferred_element_type=jnp.float32
+    )[:1]
+    norm_copies = []
+
+    def send_norm(phase, base, peers):
+        for at, offs in enumerate(peers):
+            copy = pltpu.make_async_remote_copy(
+                src_ref=norm_send.at[phase],
+                dst_ref=norm_recv.at[base + at],
+                send_sem=norm_out_sems.at[base + at],
+                recv_sem=norm_in_sems.at[base + at],
+                device_id=device(offs),
+            )
+            copy.start()
+            norm_copies.append(copy)
+
+    norm_send[0] = own_norm
+    send_norm(0, 0, first)
+
+    for t in range(slices):
+        if t == slices - 1:
+            make_tiles(t)
+        send_tiles(t)
+
+    if second:
+        for at, copy in enumerate(norm_copies):
+            copy.wait_recv()
+            own_norm = own_norm + norm_recv[at]
+        norm_send[1] = own_norm
+        send_norm(1, len(first), second)
 
     for t in range(slices):
         owns[t].wait()
@@ -214,14 +231,15 @@
             for r in range(rows_own):
                 row = p * rows_own + r
                 out_ref[p, pl.ds(t, 1), pl.ds(r * LANES, LANES)] = total[row : row + 1]
-    for off in range(1, n_ta):
-        norm_ta_copies[off - 1].wait_recv()
-        own_norm = own_norm + norm_ta_recv[off - 1]
+    landed_from = len(first) if second else 0
+    for copy in norm_copies[landed_from:]:
+        copy.wait_recv()
+    own_norm = own_norm + jnp.sum(norm_recv[landed_from:], axis=0)
     cells = 1.0 * spins * colors * slices * n_ta * sites * n_sa
     own_norm = own_norm / cells
     for s in range(srcs):
         norm_ref[pl.ds(s, 1), :] = own_norm[:, s * cols : (s + 1) * cols]
-    for copy in norm_sa_copies + norm_ta_copies:
+    for copy in norm_copies:
         copy.wait_send()
     for copy in copies.values():
         copy.wait_send()
@@ -246,6 +264,7 @@
     blocks = sites // LANES
     inner = colors * sites
     rows = parts * (width // LANES)
+    norm_peers = n_ta * n_sa - 1 if n_ta * n_sa <= DIRECT else n_ta + n_sa - 2
     f32, bf16 = jnp.float32, jnp.bfloat16
     dma = pltpu.SemaphoreType.DMA
     tiles, norms = pl.pallas_call(
@@ -274,10 +293,8 @@
             pltpu.VMEM((slices, parts, eigs * columns // LANES, LANES), f32),
             pltpu.VMEM((slices, n_sa * rows, LANES), f32),
             pltpu.VMEM((slices, n_sa * rows, LANES), f32),
-            pltpu.VMEM((1, LANES), f32),
-            pltpu.VMEM((n_sa - 1, 1, LANES), f32),
-            pltpu.VMEM((1, LANES), f32),
-            pltpu.VMEM((n_ta - 1, 1, LANES), f32),
+            pltpu.VMEM((2, 1, LANES), f32),
+            pltpu.VMEM((norm_peers, 1, LANES), f32),
             pltpu.SMEM((srcs,), jnp.int32),
             pltpu.SMEM((srcs, cols), jnp.int32),
             dma((2,)),
@@ -286,10 +303,8 @@
             dma((slices * colors * blocks,)),
             dma((slices, n_sa - 1)),
             dma((slices, n_sa - 1)),
-            dma((n_sa - 1,)),
-            dma((n_sa - 1,)),
-            dma((n_ta - 1,)),
-            dma((n_ta - 1,)),
+            dma((norm_peers,)),
+            dma((norm_peers,)),
         ],
         compiler_params=pltpu.CompilerParams(collective_id=0, has_side_effects=True),
     )(eig_view, sol_view, source_times, spin_dilution)

time: 17.1 us -> 16.5 us (0.965)
  Pallas kernels: 16.3 us -> 15.7 us
    pallas_call x1, Pallas kernels: 15 us -> 14.4 us  [on_device(): pl.pallas_call(functools.partial(kernel, dims), out_shape=(jax.ShapeDtype...]
where the time goes in v3:
time: 16.5 us; the launch traced here: 16.3 us
  Pallas kernels  15.7 us (95%)
  between operations  0.64 us (4%)
    pallas_call x1, Pallas kernels, on_device(): pl.pallas_call(functools.partial(kernel, dims), out_shape=(jax.ShapeDtype...  14.4 us
    pallas_call x1, Pallas kernels, on_device(): pl.pallas_call(hand_over, out_shape=(jax.ShapeDtypeStruct(tiles.shape, f3...  1.31 us

profile of v3, /device:TPU:0, one launch (start us, length us, event | category | flops | bytes accessed | tf_op | source)
XLA Modules:
  0.0 16.3 jit_solution(6080713991991265448)
XLA Ops:
  0.6 14.4 %shard_map.59 = (f32[2,2,768]{2,1,0:T(2,128)}, f32[3,8]{1,0:T(4,128)}) custom-call(f32[2,2,3,64,512]{4,3,2,1,0:T(8,128)} %bitcast.5, f32[2,2,24,3,4,512]{5,4,3,2,1,0:T(4,128)} %bitcast.4, s32[3]{0:T(128)} %times_hbm.1, s32[3,8]{1,0:T(4,128)} %spin_hbm.1), custom_call_target="tpu_custom_call" | custom-call | tf_op jit(solution)/shard_map/pallas_call | solution.py:270
  15.0 1.3 %shard_map.60 = (f32[2,2,768]{2,1,0:T(2,128)}, f32[3,8]{1,0:T(4,128)}) custom-call(f32[2,2,768]{2,1,0:T(2,128)} %get-tuple-element.4.tiles_ref, f32[3,8]{1,0:T(4,128)} %get-tuple-element.5.norms_ref), custom_call_target="tpu_custom_call" | custom-call | tf_op jit(solution)/shard_map/pallas_call | solution.py:311
